TPU v7x, 32 devices: a whole 2x2x4 slice. The times are simulated.
32 devices in a mesh: py: 8 (over y, x, core), pz: 4 (over z).
Axes of the slice: x: 2, y: 2, z: 4, core: 2. Of those that a mesh axis runs over, the one named last changes fastest.
Arguments:
- velocity: float32 [3, 8, 1024, 1024], P(None, 'py', 'pz'), may hold values from -14 to 14
Outputs:
- nu_t: float32 [8, 1024, 1024], P('py', 'pz')
- filtered_velocity: bfloat16 [3, 8, 1024, 1024], P(None, 'py', None, 'pz')
All inputs are finite; a program needn't handle non-finite values.
Results may differ from a plain program's by a relative error of at most 0.012.
The roundings to bfloat16 on the way count: a program that leaves them out, or rounds other values in their place, can miss the bound.
Values may be sent and summed in bfloat16 or wider, within the bound.
A program may use at most 64 MiB of HBM per device.

v0:
```python
import math
import jax
import jax.numpy as jnp
import numpy as np
from jax import lax
from jax.sharding import PartitionSpec as P

index_pairs = ((0, 0), (1, 1), (2, 2), (0, 1), (0, 2), (1, 2))
pair_weights = (1.0, 1.0, 1.0, 2.0, 2.0, 2.0)
epsilon = 1e-06


def with_halo(x, sides, width):
    for axis, dim in sides:
        devices, length = (lax.axis_size(axis), x.shape[dim])
        up = [(i, (i + 1) % devices) for i in range(devices)]
        down = [(j, i) for i, j in up]
        last = lax.slice_in_dim(x, length - width, length, axis=dim)
        initial = lax.slice_in_dim(x, 0, width, axis=dim)
        before = lax.ppermute(last, axis, up)
        after = lax.ppermute(initial, axis, down)
        x = jnp.concatenate([before, x, after], axis=dim)
    return x


def filter_table(length):
    offsets = np.arange(length, dtype=np.int64)
    wavenumbers = np.arange(1, length // 4, dtype=np.int64)
    phase = offsets[:, None] * wavenumbers[None, :] % length
    kernel = (1.0 + 2.0 * np.cos(phase * (2.0 * math.pi / length)).sum(axis=1)) / length
    kernel = kernel.astype(np.float32)
    lagged = (offsets[:, None] - offsets[None, :]) % length
    return jnp.asarray(kernel[lagged], dtype=jnp.float32).astype(jnp.bfloat16)


def seal_walls(padded):
    device_index = lax.axis_index("py")
    last_index = lax.axis_size("py") - 1
    lower_rim = jnp.where(device_index == 0, jnp.zeros_like(padded[:, :1]), padded[:, :1])
    upper_rim = jnp.where(
        device_index == last_index, jnp.zeros_like(padded[:, -1:]), padded[:, -1:]
    )
    return jnp.concatenate([lower_rim, padded[:, 1:-1], upper_rim], axis=1)


def derivatives(padded, rim_axis):
    padded = padded.astype(jnp.float32)
    if rim_axis == 2:
        interior = padded[:, 1:-1, 1:-1, :]
        slope_rim = (padded[:, 1:-1, 2:, :] - padded[:, 1:-1, :-2, :]) * 0.5
        slope_roll = (jnp.roll(interior, -1, 3) - jnp.roll(interior, 1, 3)) * 0.5
        slope_y = (padded[:, 2:, 1:-1, :] - padded[:, :-2, 1:-1, :]) * 0.5
        return (slope_roll, slope_y, slope_rim)
    interior = padded[:, 1:-1, :, 1:-1]
    slope_rim = (padded[:, 1:-1, :, 2:] - padded[:, 1:-1, :, :-2]) * 0.5
    slope_roll = (jnp.roll(interior, -1, 2) - jnp.roll(interior, 1, 2)) * 0.5
    slope_y = (padded[:, 2:, :, 1:-1] - padded[:, :-2, :, 1:-1]) * 0.5
    return (slope_rim, slope_y, slope_roll)


def strain(gradients):
    strain_parts = [0.5 * (gradients[b][a] + gradients[a][b]) for a, b in index_pairs]
    squares_sum = pair_weights[0] * strain_parts[0] * strain_parts[0]
    for weight, part_value in zip(pair_weights[1:], strain_parts[1:]):
        squares_sum = squares_sum + weight * part_value * part_value
    return (strain_parts, jnp.sqrt(2.0 * squares_sum))


def lilly_sums(filtered, padded_hat, rim_axis):
    hat_parts, magnitude_hat = strain(derivatives(padded_hat, rim_axis))
    smooth_velocity = filtered[:3].astype(jnp.float32)
    numerator = jnp.zeros_like(magnitude_hat)
    denominator = jnp.zeros_like(magnitude_hat)
    for pair_index, (a, b) in enumerate(index_pairs):
        leonard = (
            filtered[3 + pair_index].astype(jnp.float32) - smooth_velocity[a] * smooth_velocity[b]
        )
        model_term = (
            filtered[9 + pair_index].astype(jnp.float32)
            - 4.0 * magnitude_hat * hat_parts[pair_index]
        )
        numerator = numerator + pair_weights[pair_index] * leonard * model_term
        denominator = denominator + pair_weights[pair_index] * model_term * model_term
    return (jnp.sum(numerator, axis=(1, 2)), jnp.sum(denominator, axis=(1, 2)))


def body(velocity):
    padded = with_halo(velocity, (("py", 1), ("pz", 2)), 1)
    strain_parts, magnitude = strain(derivatives(seal_walls(padded), 2))
    pieces = [velocity[a].astype(jnp.bfloat16) for a in range(3)]
    pieces = pieces + [(velocity[a] * velocity[b]).astype(jnp.bfloat16) for a, b in index_pairs]
    pieces = pieces + [(magnitude * part_value).astype(jnp.bfloat16) for part_value in strain_parts]
    fields = jnp.stack(pieces)
    table_x = filter_table(velocity.shape[3])
    table_z = filter_table(velocity.shape[2] * lax.axis_size("pz"))
    along_x = jnp.einsum(
        "fyzx,xv->fyzv", fields, table_x, preferred_element_type=jnp.float32
    ).astype(jnp.bfloat16)
    filtered = jnp.einsum(
        "wz,fyzx->fywx",
        table_z,
        lax.all_to_all(along_x, "pz", split_axis=3, concat_axis=2, tiled=True),
        preferred_element_type=jnp.float32,
    ).astype(jnp.bfloat16)
    padded_hat = with_halo(filtered[:3], (("py", 1), ("pz", 3)), 1)
    numerator, denominator = lilly_sums(filtered, seal_walls(padded_hat), 3)
    numerator, denominator = lax.psum((numerator, denominator), "pz")
    plane_cells = velocity.shape[3] * velocity.shape[2] * lax.axis_size("pz")
    coefficient = numerator / plane_cells / (2.0 * (denominator / plane_cells + epsilon))
    nu_t = coefficient[:, None, None] * magnitude
    return (nu_t, filtered[:3])


def solution(mesh):
    in_specs = (P(None, "py", "pz", None),)
    out_specs = (P("py", "pz", None), P(None, "py", None, "pz"))
    return jax.shard_map(body, mesh=mesh, in_specs=in_specs, out_specs=out_specs, check_vma=False)
```

profile of v0, /device:TPU:0, one launch (start us, length us, event | category | flops | bytes accessed | tf_op | source)
XLA Modules:
  0.0 440.9 jit_solution(11105594624011594491)
XLA Ops:
  1.2 2.9 collective-permute-start.1
  17.3 53.1 %collective-permute-done = f32[3,1,256,1024]{3,2,1,0:T(8,128)S(1)} collective-permute-done((f32[3,1,256,1024]{3,2,1,0:T(8,128)}, f32[3,1,256,1024]{3,2,1,0:T(8,128)S(1)}, u32[]{:S(2)}, u32[]{:S(2)}) %collective-permute-start) | collective-permute-done | bytes 3145760 | tf_op jit(solution)/shard_map/ppermute | solution.py:20
  72.1 3.6 copy-done.5
  80.1 2.6 fusion.12
  83.0 5.7 %fusion.7 = (f32[3,1,256,1024]{3,2,1,0:T(8,128)S(1)}, f32[3,1,256,1024]{3,2,1,0:T(8,128)S(1)}) fusion(f32[3,3,256,1024]{3,2,1,0:T(8,128)} %copy-done.5, f32[3,3,1,1024]{3,2,1,0:T(1,128)S(1)} %collective-permute-done.2, f32[3,3,1,1024]{3,2,1,0:T(1,128)S(1)} %collective-permute-done.3, pred[]{:T(512)S(6)} %eq.9, pred[]{:T(512)S(6)} %eq.8), kind=kLoop, calls=%fused_computation.12 | loop fusion | flops 9437184 | bytes 15802370 | tf_op jit(solution)/shard_map/mul | solution.py:50
  96.1 13.8 %convert_bitcast_fusion = bf16[15,1,256,1024]{3,2,0,1:T(8,128)(2,1)} fusion(bf16[1024,1024,1]{1,0,2:T(8,128)(2,1)S(1)} %copy-done.10, bf16[15,1,256,1024]{3,2,0,1:T(8,128)(2,1)} %fusion.76), kind=kOutput, calls=%fused_computation.2 | convolution fusion | flops 8056995840 | bytes 17825792 | tf_op jit(solution)/shard_map/fyzx,xv->fyzv/dot_general | solution.py:96
  109.9 12.4 %copy.84 = bf16[15,1,256,1024]{2,0,1,3:T(8,128)(2,1)} copy(bf16[15,1,256,1024]{3,2,0,1:T(8,128)(2,1)} %convert_bitcast_fusion) | data formatting | bytes 15728640 | tf_op jit(solution)/shard_map/convert_element_type | solution.py:98
  122.4 191.8 %all_to_all.15 = bf16[15,1,256,1024]{2,0,1,3:T(8,128)(2,1)} all-to-all(bf16[15,1,256,1024]{2,0,1,3:T(8,128)(2,1)} %copy.84), channel_id=1, replica_groups=mesh['py'=8,'pz'=4] {'pz'}, dimensions={3} | all-to-all | bytes 15728640 | tf_op jit(solution)/shard_map/all_to_all | solution.py:102
  314.1 12.1 %copy.85 = bf16[15,1,256,1024]{3,2,0,1:T(8,128)(2,1)} copy(bf16[15,1,256,1024]{2,0,1,3:T(8,128)(2,1)} %all_to_all.15) | data formatting | bytes 15728640 | tf_op jit(solution)/shard_map/all_to_all | solution.py:102
  326.2 13.3 %reshape.1152 = bf16[15,1024,256]{2,1,0:T(8,128)(2,1)} reshape(bf16[15,1,256,1024]{3,2,0,1:T(8,128)(2,1)} %copy.85) | data formatting | bytes 15728640 | tf_op jit(solution)/shard_map/wz,fyzx->fywx/dot_general | solution.py:99
  339.5 12.2 %convolution_convert_fusion = bf16[15,256,1024]{2,1,0:T(8,128)(2,1)S(1)} fusion(bf16[15,1024,256]{2,1,0:T(8,128)(2,1)} %reshape.1152, bf16[1024,1024,1]{1,0,2:T(8,128)(2,1)} %constant.48), kind=kOutput, calls=%fused_computation.3 | convolution fusion | flops 8056995840 | bytes 17825792 | tf_op jit(solution)/shard_map/wz,fyzx->fywx/dot_general | solution.py:99
  351.7 2.6 slice_convert_fusion.3
  354.3 2.6 collective-permute-start.5
  356.9 34.1 %collective-permute-done.4 = bf16[3,1,1024,256]{2,3,1,0:T(8,128)(2,1)S(1)} collective-permute-done((bf16[3,1,1024,256]{2,3,1,0:T(8,128)(2,1)S(1)}, bf16[3,1,1024,256]{2,3,1,0:T(8,128)(2,1)S(1)}, u32[]{:S(2)}, u32[]{:S(2)}) %collective-permute-start.4) | collective-permute-done | bytes 1572896 | tf_op jit(solution)/shard_map/ppermute | solution.py:20
  392.7 3.3 collective-permute-start.7
  396.0 2.6 copy.99
  398.6 4.0 pad_maximum_fusion
  403.8 4.1 fusion.84
  408.0 3.2 fusion.4
  411.1 4.0 fusion.13
  415.2 4.5 %fusion.34 = (f32[]{:T(128)}, f32[1,1024,256]{1,2,0:T(8,128)S(1)}, f32[1,1024,256]{1,2,0:T(8,128)S(1)}, f32[1,1024,256]{1,2,0:T(8,128)S(1)}, f32[1,1024,256]{1,2,0:T(8,128)S(1)}) fusion(f32[3,1,1024,256]{2,3,1,0:T(8,128)S(1)} %copy-done.4, bf16[15,1,1024,256]{2,3,1,0:T(8,128)(2,1)} %bitcast.261, f32[3,1,1024,256]{2,3,1,0:T(8,128)S(1)} %get-tuple-element.19, ...), kind=kLoop, calls=%fused_computation.66 | loop fusion | flops 15204351 | bytes 16777220 | tf_op jit(solution)/shard_map/reduce_sum | solution.py:84
  419.7 2.6 fusion.55
  422.3 12.2 %all-reduce = (f32[1]{0:T(128)}, f32[1]{0:T(128)}) all-reduce(f32[1]{0:T(128)} %bitcast.54, f32[1]{0:T(128)} %bitcast.55), channel_id=1, replica_groups=mesh['py'=8,'pz'=4] {'pz'}, use_global_device_ids=true, to_apply=%region_1.2 | all-reduce | flops 2 | bytes 16 | tf_op jit(solution)/shard_map/psum | solution.py:107
  435.8 5.0 %fusion.40 = f32[1,256,1024]{2,1,0:T(8,128)} fusion(f32[]{:T(128)} %bitcast.56, f32[3,1,256,1024]{3,2,1,0:T(8,128)} %fusion.12, f32[3,1,256,1024]{3,2,1,0:T(8,128)} %copy-done.1, f32[3,1,256,1024]{3,2,1,0:T(8,128)S(1)} %get-tuple-element.21), kind=kLoop, calls=%fused_computation.72 | loop fusion | flops 6553600 | bytes 10485764 | tf_op jit(solution)/shard_map/mul | solution.py:110
  (62 shorter events, 30.4 us)
Async XLA Ops:
  0.6 9.0 %copy-start = (f32[3,1,256,1024]{3,2,1,0:T(8,128)S(1)}, f32[3,1,256,1024]{3,2,1,0:T(8,128)}, u32[]{:S(2)}) copy-start(f32[3,1,256,1024]{3,2,1,0:T(8,128)} %param.3) | copy-start | bytes 9437188
  0.6 69.7 %collective-permute-start = (f32[3,1,256,1024]{3,2,1,0:T(8,128)}, f32[3,1,256,1024]{3,2,1,0:T(8,128)S(1)}, u32[]{:S(2)}, u32[]{:S(2)}) collective-permute-start(f32[3,1,256,1024]{3,2,1,0:T(8,128)} %param.3), channel_id=1, source_target_pairs={{0,4},{4,8},{8,12},{12,16},{16,20},{20,24},{24,28},{28,0},{1,5},{5... | collective-permute-start | bytes 9437192 | tf_op jit(solution)/shard_map/ppermute | solution.py:20
  1.2 70.7 %collective-permute-start.1 = (f32[3,1,256,1024]{3,2,1,0:T(8,128)}, f32[3,1,256,1024]{3,2,1,0:T(8,128)S(1)}, u32[]{:S(2)}, u32[]{:S(2)}) collective-permute-start(f32[3,1,256,1024]{3,2,1,0:T(8,128)} %param.3), channel_id=1, source_target_pairs={{4,0},{8,4},{12,8},{16,12},{20,16},{24,20},{28,24},{0,28},{5,1},{9... | collective-permute-start | bytes 9437192 | tf_op jit(solution)/shard_map/ppermute | solution.py:21
  72.1 3.6 copy-start.5
  75.8 6.9 %collective-permute-start.2 = (f32[3,3,1,1024]{3,2,1,0:T(1,128)S(1)}, f32[3,3,1,1024]{3,2,1,0:T(1,128)S(1)}, u32[]{:S(2)}, u32[]{:S(2)}) collective-permute-start(f32[3,3,1,1024]{3,2,1,0:T(1,128)S(1)} %get-tuple-element.23), channel_id=1, source_target_pairs={{0,1},{1,2},{2,3},{3,0},{4,5},{5,6},{6,7},{7,4},{8,9},{9,10},{10,1... | collective-permute-start | bytes 110600 | tf_op jit(solution)/shard_map/ppermute | solution.py:20
  77.8 5.1 %collective-permute-start.3 = (f32[3,3,1,1024]{3,2,1,0:T(1,128)S(1)}, f32[3,3,1,1024]{3,2,1,0:T(1,128)S(1)}, u32[]{:S(2)}, u32[]{:S(2)}) collective-permute-start(f32[3,3,1,1024]{3,2,1,0:T(1,128)S(1)} %get-tuple-element.24), channel_id=1, source_target_pairs={{1,0},{2,1},{3,2},{0,3},{5,4},{6,5},{7,6},{4,7},{9,8},{10,9},{11,1... | collective-permute-start | bytes 110600 | tf_op jit(solution)/shard_map/ppermute | solution.py:21
  82.7 5.9 %copy-start.2 = (f32[3,1,256,1024]{3,2,1,0:T(8,128)S(1)}, f32[3,1,256,1024]{3,2,1,0:T(8,128)}, u32[]{:S(2)}) copy-start(f32[3,1,256,1024]{3,2,1,0:T(8,128)} %fusion.12) | copy-start | bytes 9437188
  88.6 6.4 %copy-start.1 = (f32[3,1,256,1024]{3,2,1,0:T(8,128)}, f32[3,1,256,1024]{3,2,1,0:T(8,128)S(1)}, u32[]{:S(2)}) copy-start(f32[3,1,256,1024]{3,2,1,0:T(8,128)S(1)} %get-tuple-element.22) | copy-start | bytes 9437188
  93.9 2.3 copy-start.10
  351.7 39.4 %copy-start.7 = (bf16[15,256,1024]{2,1,0:T(8,128)(2,1)}, bf16[15,256,1024]{2,1,0:T(8,128)(2,1)S(1)}, u32[]{:S(2)}) copy-start(bf16[15,256,1024]{2,1,0:T(8,128)(2,1)S(1)} %convolution_convert_fusion) | copy-start | bytes 23592964
  354.3 36.8 %copy-start.3 = (bf16[3,1,1024,256]{2,3,1,0:T(8,128)(2,1)}, bf16[3,1,1024,256]{2,3,1,0:T(8,128)(2,1)S(1)}, u32[]{:S(2)}) copy-start(bf16[3,1,1024,256]{2,3,1,0:T(8,128)(2,1)S(1)} %get-tuple-element.26) | copy-start | bytes 4718596
  354.3 36.8 %collective-permute-start.4 = (bf16[3,1,1024,256]{2,3,1,0:T(8,128)(2,1)S(1)}, bf16[3,1,1024,256]{2,3,1,0:T(8,128)(2,1)S(1)}, u32[]{:S(2)}, u32[]{:S(2)}) collective-permute-start(bf16[3,1,1024,256]{2,3,1,0:T(8,128)(2,1)S(1)} %get-tuple-element.26), channel_id=1, source_target_pairs={{0,4},{4,8},{8,12},{12,16},{16,20},{20,24},{24,28},{28,0},{1,5},{5... | collective-permute-start | bytes 4718600 | tf_op jit(solution)/shard_map/ppermute | solution.py:20
  354.3 36.8 %collective-permute-start.5 = (bf16[3,1,1024,256]{2,3,1,0:T(8,128)(2,1)S(1)}, bf16[3,1,1024,256]{2,3,1,0:T(8,128)(2,1)S(1)}, u32[]{:S(2)}, u32[]{:S(2)}) collective-permute-start(bf16[3,1,1024,256]{2,3,1,0:T(8,128)(2,1)S(1)} %get-tuple-element.26), channel_id=1, source_target_pairs={{4,0},{8,4},{12,8},{16,12},{20,16},{24,20},{28,24},{0,28},{5,1},{9... | collective-permute-start | bytes 4718600 | tf_op jit(solution)/shard_map/ppermute | solution.py:21
  391.0 1.2 copy-start.8
  391.1 1.6 copy-start.9
  392.2 6.4 %collective-permute-start.6 = (bf16[3,3,1024,1]{2,3,1,0:T(2,128)(2,1)S(1)}, bf16[3,3,1024,1]{2,3,1,0:T(2,128)(2,1)S(1)}, u32[]{:S(2)}, u32[]{:S(2)}) collective-permute-start(bf16[3,3,1024,1]{2,3,1,0:T(2,128)(2,1)S(1)} %get-tuple-element.32), channel_id=1, source_target_pairs={{0,1},{1,2},{2,3},{3,0},{4,5},{5,6},{6,7},{7,4},{8,9},{9,10},{10,1... | collective-permute-start | bytes 55304 | tf_op jit(solution)/shard_map/ppermute | solution.py:20
  392.7 5.9 %collective-permute-start.7 = (bf16[3,3,1024,1]{2,3,1,0:T(2,128)(2,1)S(1)}, bf16[3,3,1024,1]{2,3,1,0:T(2,128)(2,1)S(1)}, u32[]{:S(2)}, u32[]{:S(2)}) collective-permute-start(bf16[3,3,1024,1]{2,3,1,0:T(2,128)(2,1)S(1)} %get-tuple-element.33), channel_id=1, source_target_pairs={{1,0},{2,1},{3,2},{0,3},{5,4},{6,5},{7,6},{4,7},{9,8},{10,9},{11,1... | collective-permute-start | bytes 55304 | tf_op jit(solution)/shard_map/ppermute | solution.py:21
  411.1 4.0 copy-start.4
  411.1 8.5 %slice-start = ((s8[7864320]{0:T(1024)(128)(4,1)}), s8[4194304]{0:T(1024)(128)(4,1)S(1)}, s32[]{:S(2)}) async-start(s8[7864320]{0:T(1024)(128)(4,1)} %bitcast.263), calls=%async_computation.1 | async-start | bytes 8388608
  415.1 4.5 %copy-start.6 = (f32[3,1,1024,256]{2,3,1,0:T(8,128)S(1)}, f32[3,1,1024,256]{2,3,1,0:T(8,128)}, u32[]{:S(2)}) copy-start(f32[3,1,1024,256]{2,3,1,0:T(8,128)} %get-tuple-element.25) | copy-start | bytes 9437188
  415.2 4.5 %slice-start.1 = ((s8[7864320]{0:T(1024)(128)(4,1)}), s8[3670016]{0:T(1024)(128)(4,1)S(1)}, s32[]{:S(2)}) async-start(s8[7864320]{0:T(1024)(128)(4,1)} %bitcast.263), calls=%async_computation.2 | async-start | bytes 7340032
where the time goes:
time: 442 us; the launch traced here: 441 us
  blocking collectives  204 us (46%)
  waiting for transfers between devices  88.6 us (20%)
  local copies, waits for them, and re-layouts  57.9 us (13%)
  other arithmetic  48.5 us (11%)
  matrix products  26 us (6%)
  starting transfers between devices  13.8 us (3%)
    all_to_all x1, blocking collectives, body(): lax.all_to_all(along_x, 'pz', split_axis=3, concat_axis=2, tiled=True)  192 us
    ppermute x4, waiting for transfers between devices, with_halo(): before = lax.ppermute(last, axis, up)  87.2 us
    dot_general x1, matrix products, body(): jnp.einsum('fyzx,xv->fyzv', fields, table_x, preferred_element_type=jnp.f...  13.8 us
    dot_general x1, local copies, waits for them, and re-layouts, body(): jnp.einsum('wz,fyzx->fywx', table_z, lax.all_to_all(along_x, 'pz', split_...  13.3 us
    unnamed x32, local copies, waits for them, and re-layouts  13.3 us
    convert_element_type x1, local copies, waits for them, and re-layouts, body(): along_x = jnp.einsum('fyzx,xv->fyzv', fields, table_x, preferred_element_...  12.4 us
    psum x1, blocking collectives, body(): numerator, denominator = lax.psum((numerator, denominator), 'pz')  12.2 us
    dot_general x1, matrix products, body(): jnp.einsum('wz,fyzx->fywx', table_z, lax.all_to_all(along_x, 'pz', split_...  12.2 us
  transfers between devices with their start and end apart: 8, of which 4 were waited for; matrix products, arithmetic and copies ran while one was open for 4% of the time, Pallas kernels for 0%

commit v1 on v0

--- a/solution.py
+++ b/solution.py
@@ -99,7 +99,10 @@
     filtered = jnp.einsum(
         "wz,fyzx->fywx",
         table_z,
-        lax.all_to_all(along_x, "pz", split_axis=3, concat_axis=2, tiled=True),
+        jnp.concatenate(
+            lax.all_to_all(jnp.stack(jnp.split(along_x, lax.axis_size("pz"), axis=3)), "pz", 0, 0),
+            axis=2,
+        ),
         preferred_element_type=jnp.float32,
     ).astype(jnp.bfloat16)
     padded_hat = with_halo(filtered[:3], (("py", 1), ("pz", 3)), 1)

time: 442 us -> 393 us (0.89)
  local copies, waits for them, and re-layouts: 57.9 us -> 28.3 us
  blocking collectives: 204 us -> 189 us
  matrix products: 26 us -> 21.5 us
    all_to_all x1, blocking collectives: 192 us -> 177 us  [body(): lax.all_to_all(jnp.stack(jnp.split(along_x, lax.axis_size('pz'), axis=3))...]
    dot_general x1 -> x0, local copies, waits for them, and re-layouts: 13.3 us -> none  [body(): jnp.einsum('wz,fyzx->fywx', table_z, lax.all_to_all(along_x, 'pz', split_...]
    convert_element_type x1 -> x0, local copies, waits for them, and re-layouts: 12.4 us -> none  [body(): along_x = jnp.einsum('fyzx,xv->fyzv', fields, table_x, preferred_element_...]
    all_to_all x1 -> x0, local copies, waits for them, and re-layouts: 12.1 us -> none  [body(): lax.all_to_all(along_x, 'pz', split_axis=3, concat_axis=2, tiled=True)]
    reshape x0 -> x1, local copies, waits for them, and re-layouts: none -> 7.27 us  [body(): jnp.concatenate(lax.all_to_all(jnp.stack(jnp.split(along_x, lax.axis_size...]
  transfers between devices with their start and end apart: 8 -> 8, of which waited for: 4 -> 4; matrix products, arithmetic and copies ran while one was open for 4% -> 5% of each run, Pallas kernels for 0% -> 0%
where the time goes in v1:
time: 393 us
  blocking collectives  189 us (48%)
  waiting for transfers between devices  88.5 us (23%)
  other arithmetic  49.7 us (13%)
  local copies, waits for them, and re-layouts  28.3 us (7%)
  matrix products  21.5 us (5%)
  starting transfers between devices  14 us (4%)
    all_to_all x1, blocking collectives, body(): lax.all_to_all(jnp.stack(jnp.split(along_x, lax.axis_size('pz'), axis=3))...  177 us
    ppermute x4, waiting for transfers between devices, with_halo(): before = lax.ppermute(last, axis, up)  87.2 us
    unnamed x32, local copies, waits for them, and re-layouts  13.2 us
    psum x1, blocking collectives, body(): numerator, denominator = lax.psum((numerator, denominator), 'pz')  12.2 us
    unnamed x12, other arithmetic  11.8 us
    ppermute x4, starting transfers between devices, with_halo(): after = lax.ppermute(initial, axis, down)  11.2 us
    dot_general x1, matrix products, body(): jnp.einsum('wz,fyzx->fywx', table_z, jnp.concatenate(lax.all_to_all(jnp.s...  10.8 us
    dot_general x1, matrix products, body(): jnp.einsum('fyzx,xv->fyzv', fields, table_x, preferred_element_type=jnp.f...  10.7 us
  transfers between devices with their start and end apart: 8, of which 4 were waited for; matrix products, arithmetic and copies ran while one was open for 5% of the time, Pallas kernels for 0%

profile of v1, /device:TPU:0, one launch (start us, length us, event | category | flops | bytes accessed | tf_op | source)
XLA Modules:
  0.0 393.1 jit_solution(2099505755582235540)
XLA Ops:
  1.2 2.9 collective-permute-start.1
  4.1 2.1 fusion.62
  17.3 53.0 %collective-permute-done = f32[3,1,256,1024]{3,2,1,0:T(8,128)S(1)} collective-permute-done((f32[3,1,256,1024]{3,2,1,0:T(8,128)}, f32[3,1,256,1024]{3,2,1,0:T(8,128)S(1)}, u32[]{:S(2)}, u32[]{:S(2)}) %collective-permute-start) | collective-permute-done | bytes 3145760 | tf_op jit(solution)/shard_map/ppermute | solution.py:20
  72.1 3.7 copy-done.5
  77.9 2.3 collective-permute-start.3
  80.2 2.6 fusion.12
  83.0 5.7 %fusion.7 = (f32[3,1,256,1024]{3,2,1,0:T(8,128)S(1)}, f32[3,1,256,1024]{3,2,1,0:T(8,128)S(1)}) fusion(f32[3,3,256,1024]{3,2,1,0:T(8,128)} %copy-done.5, f32[3,3,1,1024]{3,2,1,0:T(1,128)S(1)} %collective-permute-done.2, f32[3,3,1,1024]{3,2,1,0:T(1,128)S(1)} %collective-permute-done.3, pred[]{:T(512)S(6)} %eq.9, pred[]{:T(512)S(6)} %eq.8), kind=kLoop, calls=%fused_computation.13 | loop fusion | flops 9437184 | bytes 15802370 | tf_op jit(solution)/shard_map/mul | solution.py:50
  96.2 10.7 %convert_bitcast_fusion = bf16[15,1,256,1024]{3,2,0,1:T(8,128)(2,1)S(1)} fusion(bf16[1024,1024,1]{1,0,2:T(8,128)(2,1)S(1)} %copy-done.10, bf16[15,1,256,1024]{3,2,0,1:T(8,128)(2,1)} %fusion.76), kind=kOutput, calls=%fused_computation.3 | convolution fusion | flops 8056995840 | bytes 17825792 | tf_op jit(solution)/shard_map/fyzx,xv->fyzv/dot_general | solution.py:96
  109.1 176.7 %all_to_all.5 = bf16[4,15,1,256,256]{4,3,1,2,0:T(8,128)(2,1)} all-to-all(bf16[4,15,1,256,256]{4,3,1,2,0:T(8,128)(2,1)S(1)} %pad_maximum_fusion), channel_id=1, replica_groups=mesh['py'=8,'pz'=4] {'pz'}, dimensions={0} | all-to-all | bytes 15728640 | tf_op jit(solution)/shard_map/all_to_all | solution.py:103
  285.8 7.3 %copy.52 = bf16[15,1,4,256,256]{4,3,2,0,1:T(8,128)(2,1)} copy(bf16[15,1,4,256,256]{4,3,0,1,2:T(8,128)(2,1)} %bitcast.265) | data formatting | bytes 15728640 | tf_op jit(solution)/shard_map/reshape | solution.py:102
  293.1 10.8 %convolution_convert_fusion = bf16[15,256,1024]{2,1,0:T(8,128)(2,1)S(1)} fusion(bf16[15,1024,256]{2,1,0:T(8,128)(2,1)} %bitcast.272, bf16[1024,1024,1]{1,0,2:T(8,128)(2,1)S(1)} %copy-done.10), kind=kOutput, calls=%fused_computation.4 | convolution fusion | flops 8056995840 | bytes 17825792 | tf_op jit(solution)/shard_map/wz,fyzx->fywx/dot_general | solution.py:99
  303.9 2.7 slice_convert_fusion.3
  306.6 2.6 collective-permute-start.5
  309.3 34.1 %collective-permute-done.4 = bf16[3,1,1024,256]{2,3,1,0:T(8,128)(2,1)S(1)} collective-permute-done((bf16[3,1,1024,256]{2,3,1,0:T(8,128)(2,1)S(1)}, bf16[3,1,1024,256]{2,3,1,0:T(8,128)(2,1)S(1)}, u32[]{:S(2)}, u32[]{:S(2)}) %collective-permute-start.4) | collective-permute-done | bytes 1572896 | tf_op jit(solution)/shard_map/ppermute | solution.py:20
  345.1 3.3 collective-permute-start.7
  348.4 2.6 copy.66
  351.0 4.0 %pad_maximum_fusion.1 = bf16[3,3,1024,258]{2,3,1,0:T(8,128)(2,1)S(1)} fusion(bf16[3,3,1024,1]{2,3,1,0:T(2,128)(2,1)S(1)} %collective-permute-done.7, bf16[3,1,1024,256]{2,3,1,0:T(8,128)(2,1)} %copy-done.9, bf16[3,1,1024,256]{2,3,1,0:T(8,128)(2,1)} %copy-done.3, bf16[3,1,1024,256]{2,3,1,0:T(8,128)(2,1)} %copy-done.8, ...), kind=kLoop, calls=%fused_computation.5 | loop fusion | flops 23777280 | bytes 9510912 | tf_op jit(solution)/shard_map/concatenate | solution.py:22
  356.2 3.9 fusion.84
  360.1 3.3 fusion.4
  363.4 4.0 %fusion.13 = f32[3,1,1024,256]{2,3,1,0:T(8,128)S(1)} fusion(f32[3,1,1,256]{2,3,1,0:T(8,128)S(1)} %get-tuple-element.30, f32[3,1,1023,256]{2,3,1,0:T(8,128)} %get-tuple-element.16, f32[3,1,1023,256]{2,3,1,0:T(8,128)} %get-tuple-element.15, f32[3,1,1,256]{2,3,1,0:T(8,128)S(1)} %get-tuple-element.29), kind=kLoop, calls=%fused_computation.26 | loop fusion | flops 3145728 | bytes 9437184 | tf_op jit(solution)/shard_map/mul | solution.py:56
  367.4 4.5 %fusion.34 = (f32[]{:T(128)}, f32[1,1024,256]{1,2,0:T(8,128)S(1)}, f32[1,1024,256]{1,2,0:T(8,128)S(1)}, f32[1,1024,256]{1,2,0:T(8,128)S(1)}, f32[1,1024,256]{1,2,0:T(8,128)S(1)}) fusion(f32[3,1,1024,256]{2,3,1,0:T(8,128)S(1)} %copy-done.4, bf16[15,1,1024,256]{2,3,1,0:T(8,128)(2,1)} %bitcast.267, f32[3,1,1024,256]{2,3,1,0:T(8,128)S(1)} %get-tuple-element.17, ...), kind=kLoop, calls=%fused_computation.71 | loop fusion | flops 15204351 | bytes 16777220 | tf_op jit(solution)/shard_map/reduce_sum | solution.py:84
  372.0 2.7 fusion.55
  374.7 12.2 %all-reduce = (f32[1]{0:T(128)}, f32[1]{0:T(128)}) all-reduce(f32[1]{0:T(128)} %bitcast.59, f32[1]{0:T(128)} %bitcast.60), channel_id=1, replica_groups=mesh['py'=8,'pz'=4] {'pz'}, use_global_device_ids=true, to_apply=%region_1.2 | all-reduce | flops 2 | bytes 16 | tf_op jit(solution)/shard_map/psum | solution.py:110
  388.1 4.9 %fusion.40 = f32[1,256,1024]{2,1,0:T(8,128)} fusion(f32[]{:T(128)} %bitcast.61, f32[3,1,256,1024]{3,2,1,0:T(8,128)} %fusion.12, f32[3,1,256,1024]{3,2,1,0:T(8,128)} %copy-done.1, f32[3,1,256,1024]{3,2,1,0:T(8,128)S(1)} %get-tuple-element.19), kind=kLoop, calls=%fused_computation.77 | loop fusion | flops 6553600 | bytes 10485764 | tf_op jit(solution)/shard_map/mul | solution.py:113
  (62 shorter events, 28.2 us)
Async XLA Ops:
  0.6 9.0 %copy-start = (f32[3,1,256,1024]{3,2,1,0:T(8,128)S(1)}, f32[3,1,256,1024]{3,2,1,0:T(8,128)}, u32[]{:S(2)}) copy-start(f32[3,1,256,1024]{3,2,1,0:T(8,128)} %param.3) | copy-start | bytes 9437188
  0.6 69.7 %collective-permute-start = (f32[3,1,256,1024]{3,2,1,0:T(8,128)}, f32[3,1,256,1024]{3,2,1,0:T(8,128)S(1)}, u32[]{:S(2)}, u32[]{:S(2)}) collective-permute-start(f32[3,1,256,1024]{3,2,1,0:T(8,128)} %param.3), channel_id=1, source_target_pairs={{0,4},{4,8},{8,12},{12,16},{16,20},{20,24},{24,28},{28,0},{1,5},{5... | collective-permute-start | bytes 9437192 | tf_op jit(solution)/shard_map/ppermute | solution.py:20
  1.2 70.7 %collective-permute-start.1 = (f32[3,1,256,1024]{3,2,1,0:T(8,128)}, f32[3,1,256,1024]{3,2,1,0:T(8,128)S(1)}, u32[]{:S(2)}, u32[]{:S(2)}) collective-permute-start(f32[3,1,256,1024]{3,2,1,0:T(8,128)} %param.3), channel_id=1, source_target_pairs={{4,0},{8,4},{12,8},{16,12},{20,16},{24,20},{28,24},{0,28},{5,1},{9... | collective-permute-start | bytes 9437192 | tf_op jit(solution)/shard_map/ppermute | solution.py:21
  72.1 3.7 copy-start.5
  75.8 6.9 %collective-permute-start.2 = (f32[3,3,1,1024]{3,2,1,0:T(1,128)S(1)}, f32[3,3,1,1024]{3,2,1,0:T(1,128)S(1)}, u32[]{:S(2)}, u32[]{:S(2)}) collective-permute-start(f32[3,3,1,1024]{3,2,1,0:T(1,128)S(1)} %get-tuple-element.21), channel_id=1, source_target_pairs={{0,1},{1,2},{2,3},{3,0},{4,5},{5,6},{6,7},{7,4},{8,9},{9,10},{10,1... | collective-permute-start | bytes 110600 | tf_op jit(solution)/shard_map/ppermute | solution.py:20
  77.9 5.1 %collective-permute-start.3 = (f32[3,3,1,1024]{3,2,1,0:T(1,128)S(1)}, f32[3,3,1,1024]{3,2,1,0:T(1,128)S(1)}, u32[]{:S(2)}, u32[]{:S(2)}) collective-permute-start(f32[3,3,1,1024]{3,2,1,0:T(1,128)S(1)} %get-tuple-element.22), channel_id=1, source_target_pairs={{1,0},{2,1},{3,2},{0,3},{5,4},{6,5},{7,6},{4,7},{9,8},{10,9},{11,1... | collective-permute-start | bytes 110600 | tf_op jit(solution)/shard_map/ppermute | solution.py:21
  82.8 5.9 %copy-start.2 = (f32[3,1,256,1024]{3,2,1,0:T(8,128)S(1)}, f32[3,1,256,1024]{3,2,1,0:T(8,128)}, u32[]{:S(2)}) copy-start(f32[3,1,256,1024]{3,2,1,0:T(8,128)} %fusion.12) | copy-start | bytes 9437188
  88.7 6.3 %copy-start.1 = (f32[3,1,256,1024]{3,2,1,0:T(8,128)}, f32[3,1,256,1024]{3,2,1,0:T(8,128)S(1)}, u32[]{:S(2)}) copy-start(f32[3,1,256,1024]{3,2,1,0:T(8,128)S(1)} %get-tuple-element.20) | copy-start | bytes 9437188
  93.9 2.3 copy-start.10
  303.9 39.6 %copy-start.7 = (bf16[15,256,1024]{2,1,0:T(8,128)(2,1)}, bf16[15,256,1024]{2,1,0:T(8,128)(2,1)S(1)}, u32[]{:S(2)}) copy-start(bf16[15,256,1024]{2,1,0:T(8,128)(2,1)S(1)} %convolution_convert_fusion) | copy-start | bytes 23592964
  306.6 36.8 %copy-start.3 = (bf16[3,1,1024,256]{2,3,1,0:T(8,128)(2,1)}, bf16[3,1,1024,256]{2,3,1,0:T(8,128)(2,1)S(1)}, u32[]{:S(2)}) copy-start(bf16[3,1,1024,256]{2,3,1,0:T(8,128)(2,1)S(1)} %get-tuple-element.24) | copy-start | bytes 4718596
  306.6 36.8 %collective-permute-start.4 = (bf16[3,1,1024,256]{2,3,1,0:T(8,128)(2,1)S(1)}, bf16[3,1,1024,256]{2,3,1,0:T(8,128)(2,1)S(1)}, u32[]{:S(2)}, u32[]{:S(2)}) collective-permute-start(bf16[3,1,1024,256]{2,3,1,0:T(8,128)(2,1)S(1)} %get-tuple-element.24), channel_id=1, source_target_pairs={{0,4},{4,8},{8,12},{12,16},{16,20},{20,24},{24,28},{28,0},{1,5},{5... | collective-permute-start | bytes 4718600 | tf_op jit(solution)/shard_map/ppermute | solution.py:20
  306.6 36.8 %collective-permute-start.5 = (bf16[3,1,1024,256]{2,3,1,0:T(8,128)(2,1)S(1)}, bf16[3,1,1024,256]{2,3,1,0:T(8,128)(2,1)S(1)}, u32[]{:S(2)}, u32[]{:S(2)}) collective-permute-start(bf16[3,1,1024,256]{2,3,1,0:T(8,128)(2,1)S(1)} %get-tuple-element.24), channel_id=1, source_target_pairs={{4,0},{8,4},{12,8},{16,12},{20,16},{24,20},{28,24},{0,28},{5,1},{9... | collective-permute-start | bytes 4718600 | tf_op jit(solution)/shard_map/ppermute | solution.py:21
  343.4 1.2 copy-start.8
  343.4 1.6 copy-start.9
  344.6 6.4 %collective-permute-start.6 = (bf16[3,3,1024,1]{2,3,1,0:T(2,128)(2,1)S(1)}, bf16[3,3,1024,1]{2,3,1,0:T(2,128)(2,1)S(1)}, u32[]{:S(2)}, u32[]{:S(2)}) collective-permute-start(bf16[3,3,1024,1]{2,3,1,0:T(2,128)(2,1)S(1)} %get-tuple-element.34), channel_id=1, source_target_pairs={{0,1},{1,2},{2,3},{3,0},{4,5},{5,6},{6,7},{7,4},{8,9},{9,10},{10,1... | collective-permute-start | bytes 55304 | tf_op jit(solution)/shard_map/ppermute | solution.py:20
  345.1 5.9 %collective-permute-start.7 = (bf16[3,3,1024,1]{2,3,1,0:T(2,128)(2,1)S(1)}, bf16[3,3,1024,1]{2,3,1,0:T(2,128)(2,1)S(1)}, u32[]{:S(2)}, u32[]{:S(2)}) collective-permute-start(bf16[3,3,1024,1]{2,3,1,0:T(2,128)(2,1)S(1)} %get-tuple-element.35), channel_id=1, source_target_pairs={{1,0},{2,1},{3,2},{0,3},{5,4},{6,5},{7,6},{4,7},{9,8},{10,9},{11,1... | collective-permute-start | bytes 55304 | tf_op jit(solution)/shard_map/ppermute | solution.py:21
  363.4 4.0 %copy-start.4 = (f32[3,1,1024,256]{2,3,1,0:T(8,128)S(1)}, f32[3,1,1024,256]{2,3,1,0:T(8,128)}, u32[]{:S(2)}) copy-start(f32[3,1,1024,256]{2,3,1,0:T(8,128)} %get-tuple-element.18) | copy-start | bytes 9437188
  363.4 8.5 %slice-start = ((s8[7864320]{0:T(1024)(128)(4,1)}), s8[4194304]{0:T(1024)(128)(4,1)S(1)}, s32[]{:S(2)}) async-start(s8[7864320]{0:T(1024)(128)(4,1)} %bitcast.269), calls=%async_computation.1 | async-start | bytes 8388608
  367.4 4.5 %copy-start.6 = (f32[3,1,1024,256]{2,3,1,0:T(8,128)S(1)}, f32[3,1,1024,256]{2,3,1,0:T(8,128)}, u32[]{:S(2)}) copy-start(f32[3,1,1024,256]{2,3,1,0:T(8,128)} %get-tuple-element.23) | copy-start | bytes 9437188
  367.4 4.5 %slice-start.1 = ((s8[7864320]{0:T(1024)(128)(4,1)}), s8[3670016]{0:T(1024)(128)(4,1)S(1)}, s32[]{:S(2)}) async-start(s8[7864320]{0:T(1024)(128)(4,1)} %bitcast.269), calls=%async_computation.2 | async-start | bytes 7340032
